TPU v7x, 32 devices: a whole 2x2x4 slice. The times are simulated.
32 devices in a mesh: src: 8 (over z, core), tgt: 4 (over y, x).
Axes of the slice: x: 2, y: 2, z: 4, core: 2. Of those that a mesh axis runs over, the one named last changes fastest.
Arguments:
- sources: float32 [64, 128, 4096], P(None, None, ('src', 'tgt')), may hold values from -6 to 6
- source_interp: float32 [128, 32, 4096], P(None, None, ('src', 'tgt')), may hold values from -0.5 to 0.5
- target_interp: float32 [128, 32, 4096], P(None, None, ('src', 'tgt')), may hold values from -1 to 1
- transfer: float32 [7, 32, 64, 4096], P(None, None, None, ('src', 'tgt')), may hold values from -0.75 to 0.75
Outputs:
- targets: float32 [64, 128, 4096], P(None, None, ('src', 'tgt'))
All inputs are finite; a program needn't handle non-finite values.
Results may differ from a plain program's by a relative error of at most 0.00017.
Values sent between devices are 32-bit elements; how exact they have to be, the bound alone decides.
A program may use at most 128 MiB of HBM per device.

v0:
```python
import jax
import jax.numpy as jnp
from jax import lax
from jax.sharding import PartitionSpec as P


def from_partner(value, axis, bit):
    mask = 2**bit
    pairs = [(source, source ^ mask) for source in range(lax.axis_size(axis))]
    return lax.ppermute(value, axis, pairs)


def flip_axis(values, axis, half):
    shape = values.shape
    length = shape[axis]
    split = shape[:axis] + (length // (2 * half), 2, half) + shape[axis + 1 :]
    return jnp.flip(values.reshape(split), axis + 1).reshape(shape)


def mixing(weight, coeffs):
    return jnp.einsum("gkj,gjr->gkr", weight, coeffs, precision=lax.Precision.HIGHEST)


def body(sources, source_interp, target_interp, transfer):
    rank = source_interp.shape[1]
    n_src = lax.axis_size("src")
    n_tgt = lax.axis_size("tgt")
    src_bits = n_src.bit_length() - 1
    tgt_bits = n_tgt.bit_length() - 1
    local_levels = transfer.shape[0] - src_bits - tgt_bits
    coeffs = jnp.einsum("bkg,rbg->gkr", source_interp, sources, precision=lax.Precision.HIGHEST)
    weights_lead = jnp.transpose(transfer, (3, 0, 1, 2))
    for depth in range(local_levels):
        weight = weights_lead[:, depth]
        partner = flip_axis(coeffs, 0, 1 << depth)
        coeffs = mixing(weight[..., :rank], coeffs) + mixing(weight[..., rank:], partner)
    src_weights = weights_lead[:, local_levels : local_levels + src_bits]
    tgt_weights = weights_lead[:, local_levels + src_bits :]
    for bit_pos in range(src_bits):
        weight = src_weights[:, bit_pos]
        own_part = mixing(weight[..., :rank], coeffs)
        partner = from_partner(coeffs, "src", bit_pos)
        coeffs = own_part + mixing(weight[..., rank:], partner)
    for bit_pos in range(tgt_bits):
        weight = tgt_weights[:, bit_pos]
        own_part = mixing(weight[..., :rank], coeffs)
        partner = from_partner(coeffs, "tgt", bit_pos)
        coeffs = own_part + mixing(weight[..., rank:], partner)
    return jnp.einsum("bkg,gkr->rbg", target_interp, coeffs, precision=lax.Precision.HIGHEST)


def solution(mesh):
    placed = (
        P(None, None, ("src", "tgt")),
        P(None, None, ("src", "tgt")),
        P(None, None, ("src", "tgt")),
        P(None, None, None, ("src", "tgt")),
    )
    return jax.shard_map(
        body, mesh=mesh, in_specs=placed, out_specs=P(None, None, ("src", "tgt")), check_vma=False
    )
```

profile of v0, /device:TPU:0, one launch (start us, length us, event | category | flops | bytes accessed | tf_op | source)
XLA Modules:
  0.0 273.9 jit_solution(13264103723900903639)
XLA Ops:
  0.0 14.5 %copy.12 = f32[7,32,64,128]{2,1,3,0:T(8,128)} copy(f32[7,32,64,128]{3,2,1,0:T(8,128)} %param.7) | data formatting | bytes 14680064 | tf_op args[3]
  14.5 11.0 %slice_bitcast_fusion = (f32[128,32,64]{2,1,0:T(8,128)S(1)}, f32[128,32,64]{2,1,0:T(8,128)}, f32[128,32,64]{2,1,0:T(8,128)}, f32[128,32,64]{2,1,0:T(8,128)}, f32...) fusion(f32[128,7,32,64]{3,2,0,1:T(8,128)} %bitcast.45), kind=kLoop, calls=%fused_computation.5 | loop fusion | bytes 14680064 | tf_op jit(solution)/shard_map/squeeze | solution.py:45
  25.5 5.3 %copy.11 = f32[64,128,128]{1,0,2:T(8,128)} copy(f32[64,128,128]{2,1,0:T(8,128)} %param.4) | data formatting | bytes 8388608 | tf_op args[0]
  30.8 3.8 %copy.10 = f32[128,32,128]{0,1,2:T(8,128)} copy(f32[128,32,128]{2,1,0:T(8,128)} %param.5) | data formatting | bytes 4194304 | tf_op args[1]
  34.7 10.8 %fusion.47 = f32[128,32,64]{2,1,0:T(8,128)} fusion(f32[128,32,128]{0,1,2:T(8,128)} %copy.10, f32[64,128,128]{1,0,2:T(8,128)} %copy.11), kind=kOutput, calls=%fused_computation.43 | convolution fusion | flops 402653184 | bytes 7340032 | tf_op jit(solution)/shard_map/bkg,rbg->gkr/dot_general | solution.py:31
  45.4 3.1 %rev.8 = f32[64,2,1,32,64]{4,3,1,0,2:T(8,128)} reverse(f32[64,2,1,32,64]{4,3,1,0,2:T(8,128)} %bitcast.52), dimensions={1} | reverse | bytes 2097152 | tf_op jit(solution)/shard_map/jit(_flip)/rev | solution.py:17
  48.5 0.0 copy-start.1
  48.5 0.0 copy-start.3
  48.5 4.7 %fusion.24 = f32[128,64,32]{1,2,0:T(8,128)S(1)} fusion(f32[128,32,64]{2,1,0:T(8,128)} %bitcast.53, f32[128,32,64]{2,1,0:T(8,128)} %get-tuple-element.11), kind=kOutput, calls=%fused_computation.31 | convolution fusion | flops 100663296 | bytes 3145728 | tf_op jit(solution)/shard_map/gkj,gjr->gkr/dot_general | solution.py:21
  53.2 0.0 copy-done.1
  53.2 0.0 copy-done.3
  53.2 3.5 %fusion.29 = f32[128,64,32]{1,2,0:T(8,128)} fusion(f32[128,64,32]{1,2,0:T(8,128)S(1)} %fusion.24, f32[128,32,64]{2,1,0:T(8,128)S(1)} %copy-done.3, f32[128,32,64]{2,1,0:T(8,128)S(1)} %copy-done.1), kind=kOutput, calls=%fused_computation.37 | convolution fusion | flops 100925440 | bytes 4194304 | tf_op jit(solution)/shard_map/gkj,gjr->gkr/dot_general | solution.py:21
  56.8 3.2 %rev.9 = f32[32,2,2,32,64]{4,3,2,1,0:T(8,128)} reverse(f32[32,2,2,32,64]{4,3,2,1,0:T(8,128)} %bitcast.51), dimensions={1} | reverse | bytes 2097152 | tf_op jit(solution)/shard_map/jit(_flip)/rev | solution.py:17
  60.0 0.0 copy-start
  60.0 0.0 copy-start.2
  60.0 4.8 %fusion.20 = f32[128,64,32]{1,2,0:T(8,128)S(1)} fusion(f32[128,32,64]{2,1,0:T(8,128)} %bitcast.54, f32[128,32,64]{2,1,0:T(8,128)} %get-tuple-element.10), kind=kOutput, calls=%fused_computation.26 | convolution fusion | flops 100663296 | bytes 3145728 | tf_op jit(solution)/shard_map/gkj,gjr->gkr/dot_general | solution.py:21
  64.8 0.0 copy-done
  64.8 0.0 copy-done.2
  64.9 3.5 %fusion.32 = f32[128,64,32]{1,2,0:T(8,128)} fusion(f32[128,64,32]{1,2,0:T(8,128)S(1)} %fusion.20, f32[128,64,32]{1,2,0:T(8,128)S(1)} %copy-done.2, f32[128,32,64]{2,1,0:T(8,128)S(1)} %copy-done), kind=kOutput, calls=%fused_computation.38 | convolution fusion | flops 100925440 | bytes 4194304 | tf_op jit(solution)/shard_map/gkj,gjr->gkr/dot_general | solution.py:21
  68.4 3.7 %copy.13 = f32[128,32,64]{0,2,1:T(8,128)} copy(f32[128,32,64]{2,1,0:T(8,128)} %bitcast.47) | data formatting | bytes 2097152 | tf_op jit(solution)/shard_map/add | solution.py:36
  72.1 0.5 collective-permute-start
  72.5 5.6 %fusion.18 = f32[128,64,32]{1,2,0:T(8,128)} fusion(f32[128,64,32]{1,2,0:T(8,128)} %fusion.32, f32[128,32,64]{2,1,0:T(8,128)} %get-tuple-element.9), kind=kOutput, calls=%fused_computation.23 | convolution fusion | flops 100663296 | bytes 3145728 | tf_op jit(solution)/shard_map/gkj,gjr->gkr/dot_general | solution.py:21
  78.1 0.0 collective-permute-done
  78.1 2.8 %copy.14 = f32[128,32,64]{2,1,0:T(8,128)} copy(f32[128,32,64]{0,2,1:T(8,128)S(1)} %collective-permute-done) | data formatting | bytes 2097152 | tf_op jit(solution)/shard_map/ppermute | solution.py:10
  81.0 6.4 %fusion.35 = f32[128,64,32]{1,2,0:T(8,128)} fusion(f32[128,64,32]{1,2,0:T(8,128)} %fusion.18, f32[128,32,64]{2,1,0:T(8,128)} %copy.14, f32[128,32,64]{2,1,0:T(8,128)} %get-tuple-element.9), kind=kOutput, calls=%fused_computation.39 | convolution fusion | flops 100925440 | bytes 4194304 | tf_op jit(solution)/shard_map/gkj,gjr->gkr/dot_general | solution.py:21
  87.4 3.7 %copy.15 = f32[128,32,64]{0,2,1:T(8,128)} copy(f32[128,32,64]{2,1,0:T(8,128)} %bitcast.48) | data formatting | bytes 2097152 | tf_op jit(solution)/shard_map/add | solution.py:43
  91.0 2.6 collective-permute-start.1
  93.6 5.8 %fusion.14 = f32[128,64,32]{1,2,0:T(8,128)} fusion(f32[128,64,32]{1,2,0:T(8,128)} %fusion.35, f32[128,32,64]{2,1,0:T(8,128)} %get-tuple-element.8), kind=kOutput, calls=%fused_computation.18 | convolution fusion | flops 100663296 | bytes 3145728 | tf_op jit(solution)/shard_map/gkj,gjr->gkr/dot_general | solution.py:21
  99.4 18.2 %collective-permute-done.1 = f32[128,32,64]{0,2,1:T(8,128)S(1)} collective-permute-done((f32[128,32,64]{0,2,1:T(8,128)}, f32[128,32,64]{0,2,1:T(8,128)S(1)}, u32[]{:S(2)}, u32[]{:S(2)}) %collective-permute-start.1) | collective-permute-done | bytes 1048608 | tf_op jit(solution)/shard_map/ppermute | solution.py:10
  117.6 2.8 %copy.16 = f32[128,32,64]{2,1,0:T(8,128)} copy(f32[128,32,64]{0,2,1:T(8,128)S(1)} %collective-permute-done.1) | data formatting | bytes 2097152 | tf_op jit(solution)/shard_map/ppermute | solution.py:10
  120.5 6.4 %fusion.38 = f32[128,64,32]{1,2,0:T(8,128)} fusion(f32[128,64,32]{1,2,0:T(8,128)} %fusion.14, f32[128,32,64]{2,1,0:T(8,128)} %copy.16, f32[128,32,64]{2,1,0:T(8,128)} %get-tuple-element.8), kind=kOutput, calls=%fused_computation.40 | convolution fusion | flops 100925440 | bytes 4194304 | tf_op jit(solution)/shard_map/gkj,gjr->gkr/dot_general | solution.py:21
  126.9 3.7 %copy.17 = f32[128,32,64]{0,2,1:T(8,128)} copy(f32[128,32,64]{2,1,0:T(8,128)} %bitcast.49) | data formatting | bytes 2097152 | tf_op jit(solution)/shard_map/add | solution.py:43
  130.5 2.8 %collective-permute-start.2 = (f32[128,32,64]{0,2,1:T(8,128)}, f32[128,32,64]{0,2,1:T(8,128)S(1)}, u32[]{:S(2)}, u32[]{:S(2)}) collective-permute-start(f32[128,32,64]{0,2,1:T(8,128)} %copy.17), channel_id=1, source_target_pairs={{0,16},{4,20},{8,24},{12,28},{16,0},{20,4},{24,8},{28,12},{1,17},{... | collective-permute-start | bytes 3145736 | tf_op jit(solution)/shard_map/ppermute | solution.py:10
  133.3 5.6 %fusion.10 = f32[128,64,32]{1,2,0:T(8,128)} fusion(f32[128,64,32]{1,2,0:T(8,128)} %fusion.38, f32[128,32,64]{2,1,0:T(8,128)} %get-tuple-element.7), kind=kOutput, calls=%fused_computation.13 | convolution fusion | flops 100663296 | bytes 3145728 | tf_op jit(solution)/shard_map/gkj,gjr->gkr/dot_general | solution.py:21
  138.9 40.2 %collective-permute-done.2 = f32[128,32,64]{0,2,1:T(8,128)S(1)} collective-permute-done((f32[128,32,64]{0,2,1:T(8,128)}, f32[128,32,64]{0,2,1:T(8,128)S(1)}, u32[]{:S(2)}, u32[]{:S(2)}) %collective-permute-start.2) | collective-permute-done | bytes 1048608 | tf_op jit(solution)/shard_map/ppermute | solution.py:10
  179.1 2.8 %copy.18 = f32[128,32,64]{2,1,0:T(8,128)} copy(f32[128,32,64]{0,2,1:T(8,128)S(1)} %collective-permute-done.2) | data formatting | bytes 2097152 | tf_op jit(solution)/shard_map/ppermute | solution.py:10
  181.9 6.4 %fusion.41 = f32[128,64,32]{1,2,0:T(8,128)} fusion(f32[128,64,32]{1,2,0:T(8,128)} %fusion.10, f32[128,32,64]{2,1,0:T(8,128)} %copy.18, f32[128,32,64]{2,1,0:T(8,128)} %get-tuple-element.7), kind=kOutput, calls=%fused_computation.41 | convolution fusion | flops 100925440 | bytes 4194304 | tf_op jit(solution)/shard_map/gkj,gjr->gkr/dot_general | solution.py:21
  188.3 4.1 %copy.19 = f32[128,32,64]{0,2,1:T(8,128)} copy(f32[128,32,64]{2,1,0:T(8,128)} %bitcast.50) | data formatting | bytes 2097152 | tf_op jit(solution)/shard_map/add | solution.py:43
  192.4 1.4 collective-permute-start.3
  193.8 5.6 %fusion.6 = f32[128,64,32]{1,2,0:T(8,128)} fusion(f32[128,64,32]{1,2,0:T(8,128)} %fusion.41, f32[128,32,64]{2,1,0:T(8,128)} %get-tuple-element.6), kind=kOutput, calls=%fused_computation.8 | convolution fusion | flops 100663296 | bytes 3145728 | tf_op jit(solution)/shard_map/gkj,gjr->gkr/dot_general | solution.py:21
  199.4 17.4 %collective-permute-done.3 = f32[128,32,64]{0,2,1:T(8,128)S(1)} collective-permute-done((f32[128,32,64]{0,2,1:T(8,128)}, f32[128,32,64]{0,2,1:T(8,128)S(1)}, u32[]{:S(2)}, u32[]{:S(2)}) %collective-permute-start.3) | collective-permute-done | bytes 1048608 | tf_op jit(solution)/shard_map/ppermute | solution.py:10
  216.8 2.8 %copy.20 = f32[128,32,64]{2,1,0:T(8,128)} copy(f32[128,32,64]{0,2,1:T(8,128)S(1)} %collective-permute-done.3) | data formatting | bytes 2097152 | tf_op jit(solution)/shard_map/ppermute | solution.py:10
  219.6 6.4 %fusion.44 = f32[128,64,32]{1,2,0:T(8,128)} fusion(f32[128,64,32]{1,2,0:T(8,128)} %fusion.6, f32[128,32,64]{2,1,0:T(8,128)} %copy.20, f32[128,32,64]{2,1,0:T(8,128)} %get-tuple-element.6), kind=kOutput, calls=%fused_computation.42 | convolution fusion | flops 100925440 | bytes 4194304 | tf_op jit(solution)/shard_map/gkj,gjr->gkr/dot_general | solution.py:21
  226.0 3.6 %copy.21 = f32[128,32,64]{0,2,1:T(8,128)} copy(f32[128,32,64]{2,1,0:T(8,128)} %bitcast.46) | data formatting | bytes 2097152 | tf_op jit(solution)/shard_map/add | solution.py:48
  229.7 1.3 collective-permute-start.4
  230.9 3.5 %copy.22 = f32[128,32,128]{0,1,2:T(8,128)} copy(f32[128,32,128]{2,1,0:T(8,128)} %param.6) | data formatting | bytes 4194304 | tf_op args[2]
  234.5 5.0 %fusion.2 = f32[128,64,32]{1,2,0:T(8,128)} fusion(f32[128,64,32]{1,2,0:T(8,128)} %fusion.44, f32[128,32,64]{2,1,0:T(8,128)S(1)} %get-tuple-element.5), kind=kOutput, calls=%fused_computation.3 | convolution fusion | flops 100663296 | bytes 3145728 | tf_op jit(solution)/shard_map/gkj,gjr->gkr/dot_general | solution.py:21
  239.4 13.8 %collective-permute-done.4 = f32[128,32,64]{0,2,1:T(8,128)S(1)} collective-permute-done((f32[128,32,64]{0,2,1:T(8,128)}, f32[128,32,64]{0,2,1:T(8,128)S(1)}, u32[]{:S(2)}, u32[]{:S(2)}) %collective-permute-start.4) | collective-permute-done | bytes 1048608 | tf_op jit(solution)/shard_map/ppermute | solution.py:10
  253.2 2.8 %copy.24 = f32[128,32,64]{2,1,0:T(8,128)} copy(f32[128,32,64]{0,2,1:T(8,128)S(1)} %collective-permute-done.4) | data formatting | bytes 2097152 | tf_op jit(solution)/shard_map/ppermute | solution.py:10
  256.0 0.0 copy-start.4
  256.0 0.0 copy-start.5
  256.0 4.0 %fusion = f32[128,64,32]{1,2,0:T(8,128)S(1)} fusion(f32[128,32,64]{2,1,0:T(8,128)} %copy.24, f32[128,32,64]{2,1,0:T(8,128)S(1)} %get-tuple-element.5), kind=kOutput, calls=%fused_computation.1 | convolution fusion | flops 100663296 | bytes 3145728 | tf_op jit(solution)/shard_map/gkj,gjr->gkr/dot_general | solution.py:21
  260.0 0.0 copy-done.4
  260.0 0.0 copy-done.5
  260.0 8.2 %convolution_bitcast_fusion = f32[64,128,128]{1,0,2:T(8,128)} fusion(f32[128,32,128]{0,1,2:T(8,128)S(1)} %copy-done.5, f32[128,64,32]{1,2,0:T(8,128)S(1)} %copy-done.4, f32[128,64,32]{1,2,0:T(8,128)S(1)} %fusion), kind=kOutput, calls=%fused_computation | convolution fusion | flops 402915328 | bytes 8388608 | tf_op jit(solution)/shard_map/bkg,gkr->rbg/dot_general | solution.py:49
  268.3 5.4 %copy.23 = f32[64,128,128]{2,1,0:T(8,128)} copy(f32[64,128,128]{1,0,2:T(8,128)} %convolution_bitcast_fusion) | data formatting | bytes 8388608 | tf_op jit(solution)/shard_map/bkg,gkr->rbg/transpose | solution.py:49
Async XLA Ops:
  48.5 4.7 %copy-start.1 = (f32[128,32,64]{2,1,0:T(8,128)S(1)}, f32[128,32,64]{2,1,0:T(8,128)}, u32[]{:S(2)}) copy-start(f32[128,32,64]{2,1,0:T(8,128)} %get-tuple-element.11) | copy-start | bytes 3145732
  48.5 4.7 %copy-start.3 = (f32[128,32,64]{2,1,0:T(8,128)S(1)}, f32[128,32,64]{2,1,0:T(8,128)}, u32[]{:S(2)}) copy-start(f32[128,32,64]{2,1,0:T(8,128)} %fusion.47) | copy-start | bytes 3145732
  60.0 4.9 %copy-start = (f32[128,32,64]{2,1,0:T(8,128)S(1)}, f32[128,32,64]{2,1,0:T(8,128)}, u32[]{:S(2)}) copy-start(f32[128,32,64]{2,1,0:T(8,128)} %get-tuple-element.10) | copy-start | bytes 3145732
  60.0 4.9 %copy-start.2 = (f32[128,64,32]{1,2,0:T(8,128)S(1)}, f32[128,64,32]{1,2,0:T(8,128)}, u32[]{:S(2)}) copy-start(f32[128,64,32]{1,2,0:T(8,128)} %fusion.29) | copy-start | bytes 3145732
  72.1 6.1 %collective-permute-start = (f32[128,32,64]{0,2,1:T(8,128)}, f32[128,32,64]{0,2,1:T(8,128)S(1)}, u32[]{:S(2)}, u32[]{:S(2)}) collective-permute-start(f32[128,32,64]{0,2,1:T(8,128)} %copy.13), channel_id=1, source_target_pairs={{0,4},{4,0},{8,12},{12,8},{16,20},{20,16},{24,28},{28,24},{1,5},{5... | collective-permute-start | bytes 3145736 | tf_op jit(solution)/shard_map/ppermute | solution.py:10
  91.0 26.6 %collective-permute-start.1 = (f32[128,32,64]{0,2,1:T(8,128)}, f32[128,32,64]{0,2,1:T(8,128)S(1)}, u32[]{:S(2)}, u32[]{:S(2)}) collective-permute-start(f32[128,32,64]{0,2,1:T(8,128)} %copy.15), channel_id=1, source_target_pairs={{0,8},{4,12},{8,0},{12,4},{16,24},{20,28},{24,16},{28,20},{1,9},{5... | collective-permute-start | bytes 3145736 | tf_op jit(solution)/shard_map/ppermute | solution.py:10
  130.5 48.6 %collective-permute-start.2 = (f32[128,32,64]{0,2,1:T(8,128)}, f32[128,32,64]{0,2,1:T(8,128)S(1)}, u32[]{:S(2)}, u32[]{:S(2)}) collective-permute-start(f32[128,32,64]{0,2,1:T(8,128)} %copy.17), channel_id=1, source_target_pairs={{0,16},{4,20},{8,24},{12,28},{16,0},{20,4},{24,8},{28,12},{1,17},{... | collective-permute-start | bytes 3145736 | tf_op jit(solution)/shard_map/ppermute | solution.py:10
  192.4 24.4 %collective-permute-start.3 = (f32[128,32,64]{0,2,1:T(8,128)}, f32[128,32,64]{0,2,1:T(8,128)S(1)}, u32[]{:S(2)}, u32[]{:S(2)}) collective-permute-start(f32[128,32,64]{0,2,1:T(8,128)} %copy.19), channel_id=1, source_target_pairs={{0,1},{1,0},{2,3},{3,2},{4,5},{5,4},{6,7},{7,6},{8,9},{9,8},{10,11... | collective-permute-start | bytes 3145736 | tf_op jit(solution)/shard_map/ppermute | solution.py:10
  229.7 23.5 %collective-permute-start.4 = (f32[128,32,64]{0,2,1:T(8,128)}, f32[128,32,64]{0,2,1:T(8,128)S(1)}, u32[]{:S(2)}, u32[]{:S(2)}) collective-permute-start(f32[128,32,64]{0,2,1:T(8,128)} %copy.21), channel_id=1, source_target_pairs={{0,2},{1,3},{2,0},{3,1},{4,6},{5,7},{6,4},{7,5},{8,10},{9,11},{10,... | collective-permute-start | bytes 3145736 | tf_op jit(solution)/shard_map/ppermute | solution.py:10
  256.0 4.0 %copy-start.4 = (f32[128,64,32]{1,2,0:T(8,128)S(1)}, f32[128,64,32]{1,2,0:T(8,128)}, u32[]{:S(2)}) copy-start(f32[128,64,32]{1,2,0:T(8,128)} %fusion.2) | copy-start | bytes 3145732
  256.0 4.0 %copy-start.5 = (f32[128,32,128]{0,1,2:T(8,128)S(1)}, f32[128,32,128]{0,1,2:T(8,128)}, u32[]{:S(2)}) copy-start(f32[128,32,128]{0,1,2:T(8,128)} %copy.22) | copy-start | bytes 6291460
where the time goes:
time: 278 us; the launch traced here: 274 us
  matrix products  92.8 us (33%)
  waiting for transfers between devices  89.6 us (32%)
  local copies, waits for them, and re-layouts  82.6 us (30%)
  starting transfers between devices  8.47 us (3%)
    ppermute x5, waiting for transfers between devices, from_partner(): return lax.ppermute(value, axis, pairs)  89.6 us
    dot_general x14, matrix products, mixing(): jnp.einsum('gkj,gjr->gkr', weight, coeffs, precision=lax.Precision.HIGHEST)  73.8 us
    unnamed x16, local copies, waits for them, and re-layouts  27.2 us
    add x4, local copies, waits for them, and re-layouts, body(): coeffs = own_part + mixing(weight[..., rank:], partner)  15 us
    ppermute x5, local copies, waits for them, and re-layouts, from_partner(): return lax.ppermute(value, axis, pairs)  14.1 us
    squeeze x1, local copies, waits for them, and re-layouts, body(): weight = tgt_weights[:, bit_pos]  11 us
    dot_general x1, matrix products, body(): jnp.einsum('bkg,rbg->gkr', source_interp, sources, precision=lax.Precisio...  10.8 us
    ppermute x5, starting transfers between devices, from_partner(): return lax.ppermute(value, axis, pairs)  8.47 us
  transfers between devices with their start and end apart: 5, of which 4 were waited for; matrix products, arithmetic and copies ran while one was open for 11% of the time, Pallas kernels for 0%

commit v1 on v0

v1 whole, which is shorter than its diff:
```python
import functools

import jax
import jax.numpy as jnp
from jax import lax
from jax.experimental import pallas as pl
from jax.experimental.pallas import tpu as pltpu
from jax.sharding import PartitionSpec as P

ROWS = 8
TILES = 2
PAD = 8


def flip_mask(axis, bit):
    me = lax.axis_index(axis)
    half = 2**bit
    return me + half - 2 * half * ((me // half) % 2)


def mix(weight_at, source_at, store, depth, outs, tiles, block, unroll):
    def one_block(start):
        def step(outer, acc):
            acc = list(acc)
            for inner in range(unroll):
                j = outer * unroll + inner
                rows = [source_at(j, t) for t in range(tiles)]
                for i in range(block):
                    w = weight_at(start + i, j)
                    for t in range(tiles):
                        acc[i * tiles + t] = acc[i * tiles + t] + w * rows[t]
            return tuple(acc)

        zero = jnp.zeros((ROWS, 128), jnp.float32)
        acc = lax.fori_loop(0, depth // unroll, step, (zero,) * (block * tiles))
        for i in range(block):
            for t in range(tiles):
                store(start + i, t, acc[i * tiles + t])

    def body(b, carry):
        one_block(b * block)
        return carry

    lax.fori_loop(0, outs // block, body, 0)


def kernel(dims, sources, interp_in, interp_out, transfer, out,
           s_buf, si_buf, ti_buf, w_buf, c_buf, p_buf, o_buf,
           load_sem, s_sem, w_sem, o_sem, send_sem, recv_sem):
    rank, rhs, points, levels, local, partners = dims
    tiles = TILES
    width = ROWS * tiles
    chunks = rhs // width
    pitch = points + PAD

    loads_si = pltpu.make_async_copy(interp_in, si_buf, load_sem.at[0])
    loads_ti = pltpu.make_async_copy(interp_out, ti_buf, load_sem.at[1])

    def source_copy(r):
        return pltpu.make_async_copy(
            sources.at[r], s_buf.at[pl.ds(r * pitch, points)], s_sem.at[r])

    def weight_copy(n):
        return pltpu.make_async_copy(
            transfer.at[pl.ds(n * rank * 2 * rank, rank * 2 * rank)], w_buf.at[n], w_sem.at[n])

    def start_sources(r, carry):
        source_copy(r).start()
        return carry

    def wait_sources(r, carry):
        source_copy(r).wait()
        return carry

    loads_si.start()
    lax.fori_loop(0, rhs, start_sources, 0)
    for n in range(levels):
        weight_copy(n).start()
    loads_ti.start()

    barrier = pltpu.get_barrier_semaphore()
    where = [{axis: flip_mask(axis, bit)} for axis, bit in partners]
    for device in where:
        pl.semaphore_signal(barrier, inc=1, device_id=device, device_id_type=pl.DeviceIdType.MESH)
    pl.semaphore_wait(barrier, len(where))

    lane = lax.broadcasted_iota(jnp.int32, (ROWS, 128), 1)

    def at_chunk(c, k, t):
        return pl.ds(c * rank * width + k * width + t * ROWS, ROWS)

    def exchange(n, c):
        e = n - local
        part = pl.ds(c * rank * width, rank * width)
        return pltpu.make_async_remote_copy(
            src_ref=c_buf.at[n, part], dst_ref=p_buf.at[n, part],
            send_sem=send_sem.at[e, c], recv_sem=recv_sem.at[e, c],
            device_id=where[e], device_id_type=pl.DeviceIdType.MESH)

    def deliver(n, c):
        if n >= local:
            if n < levels:
                exchange(n, c).start()
            return
        half = 2**n

        def flip(k, carry):
            for t in range(tiles):
                x = c_buf[n, at_chunk(c, k, t), :]
                low = (lane // half) % 2 == 0
                p_buf[n, at_chunk(c, k, t), :] = jnp.where(
                    low, pltpu.roll(x, 128 - half, 1), pltpu.roll(x, half, 1))
            return carry

        lax.fori_loop(0, rank, flip, 0)

    def first(c):
        if c == 0:
            loads_si.wait()
        lax.fori_loop(c * width, (c + 1) * width, wait_sources, 0)

        def weight_at(k, b):
            return si_buf[pl.ds(b * rank + k, ROWS, stride=0), :]

        def source_at(b, t):
            return s_buf[pl.ds((c * width + t * ROWS) * pitch + b, ROWS, stride=pitch), :]

        def store(k, t, value):
            c_buf[0, at_chunk(c, k, t), :] = value

        mix(weight_at, source_at, store, points, rank, tiles, 32 // tiles, 4)
        deliver(0, c)

    def level(n, c):
        if c == 0:
            weight_copy(n).wait()
        if n >= local:
            exchange(n, c).wait_recv()
        block = 32 // tiles

        def body(b, carry):
            def step(outer, acc):
                acc = list(acc)
                for buf, base in ((c_buf, 0), (p_buf, rank)):
                    for inner in range(2):
                        j = outer * 2 + inner
                        rows = [buf[n, at_chunk(c, j, t), :] for t in range(tiles)]
                        for i in range(block):
                            w = w_buf[n, pl.ds((b * block + i) * 2 * rank + base + j, ROWS, stride=0), :]
                            for t in range(tiles):
                                acc[i * tiles + t] = acc[i * tiles + t] + w * rows[t]
                return tuple(acc)

            zero = jnp.zeros((ROWS, 128), jnp.float32)
            acc = lax.fori_loop(0, rank // 2, step, (zero,) * (block * tiles))
            for i in range(block):
                for t in range(tiles):
                    c_buf[n + 1, at_chunk(c, b * block + i, t), :] = acc[i * tiles + t]
            return carry

        lax.fori_loop(0, rank // block, body, 0)
        deliver(n + 1, c)

    def out_copy(r):
        return pltpu.make_async_copy(
            o_buf.at[pl.ds(r * pitch, points)], out.at[r], o_sem.at[r])

    def start_out(r, carry):
        out_copy(r).start()
        return carry

    def wait_out(r, carry):
        out_copy(r).wait()
        return carry

    def last(c):
        if c == 0:
            loads_ti.wait()

        def weight_at(b, k):
            return ti_buf[pl.ds(b * rank + k, ROWS, stride=0), :]

        def source_at(k, t):
            return c_buf[levels, at_chunk(c, k, t), :]

        def store(b, t, value):
            o_buf[pl.ds((c * width + t * ROWS) * pitch + b, ROWS, stride=pitch), :] = value

        mix(weight_at, source_at, store, rank, points, tiles, 32 // tiles, 4)
        lax.fori_loop(c * width, (c + 1) * width, start_out, 0)

    for task, c in schedule(chunks, levels, local, partners):
        if task == 0:
            first(c)
        elif task <= levels:
            level(task - 1, c)
        else:
            last(c)

    for n in range(local, levels):
        for c in range(chunks):
            exchange(n, c).wait_send()
    lax.fori_loop(0, rhs, wait_out, 0)


def schedule(chunks, levels, local, partners):
    work = [2.0] + [1.0] * levels + [2.0]
    flight = [0.0] * (levels + 2)
    links = [None] * (levels + 2)
    for e, (axis, bit) in enumerate(partners):
        flight[local + e + 1] = 0.5 if (axis == "src" and bit == 0) else 5.0
        links[local + e + 1] = (axis, bit) if axis == "tgt" or bit == 0 else axis
    busy, ready, nxt = {}, {(0, c): 0.0 for c in range(chunks)}, {c: 0 for c in range(chunks)}
    now, order = 0.0, []
    while nxt:
        open_now = [(c, t) for c, t in nxt.items() if ready[t, c] <= now]
        if not open_now:
            now = min(ready[t, c] for c, t in nxt.items())
            continue
        c, t = min(open_now)
        now += work[t]
        order.append((t, c))
        if t == levels + 1:
            del nxt[c]
            continue
        start = now
        if links[t + 1] is not None:
            start = max(now, busy.get(links[t + 1], 0.0))
            busy[links[t + 1]] = start + flight[t + 1]
        ready[t + 1, c] = start + flight[t + 1] + (0.0 if links[t + 1] is None else 1.5)
        nxt[c] = t + 1
    return order


def body(sources, source_interp, target_interp, transfer):
    rhs, points, blocks = sources.shape
    rank = source_interp.shape[1]
    levels = transfer.shape[0]
    src_bits = lax.axis_size("src").bit_length() - 1
    tgt_bits = lax.axis_size("tgt").bit_length() - 1
    local = levels - src_bits - tgt_bits
    partners = [("src", b) for b in range(src_bits)] + [("tgt", b) for b in range(tgt_bits)]
    dims = (rank, rhs, points, levels, local, partners)
    chunks = rhs // (ROWS * TILES)
    pitch = points + PAD
    f32 = jnp.float32
    any_space = pl.BlockSpec(memory_space=pl.ANY)
    return pl.pallas_call(
        functools.partial(kernel, dims),
        out_shape=jax.ShapeDtypeStruct(sources.shape, f32),
        in_specs=[any_space] * 4,
        out_specs=any_space,
        scratch_shapes=[
            pltpu.VMEM((rhs * pitch, blocks), f32),
            pltpu.VMEM((points * rank, blocks), f32),
            pltpu.VMEM((points * rank, blocks), f32),
            pltpu.VMEM((levels, rank * 2 * rank, blocks), f32),
            pltpu.VMEM((levels + 1, rhs * rank, blocks), f32),
            pltpu.VMEM((levels, rhs * rank, blocks), f32),
            pltpu.VMEM((rhs * pitch, blocks), f32),
            pltpu.SemaphoreType.DMA((2,)),
            pltpu.SemaphoreType.DMA((rhs,)),
            pltpu.SemaphoreType.DMA((levels,)),
            pltpu.SemaphoreType.DMA((rhs,)),
            pltpu.SemaphoreType.DMA((len(partners), chunks)),
            pltpu.SemaphoreType.DMA((len(partners), chunks)),
        ],
        compiler_params=pltpu.CompilerParams(
            collective_id=0, has_side_effects=True, vmem_limit_bytes=60 * 2**20),
    )(sources, source_interp.reshape(points * rank, blocks),
      target_interp.reshape(points * rank, blocks),
      transfer.reshape(levels * rank * 2 * rank, blocks))


def solution(mesh):
    placed = (
        P(None, None, ("src", "tgt")),
        P(None, None, ("src", "tgt")),
        P(None, None, ("src", "tgt")),
        P(None, None, None, ("src", "tgt")),
    )
    return jax.shard_map(
        body, mesh=mesh, in_specs=placed, out_specs=P(None, None, ("src", "tgt")), check_vma=False
    )
```

time: 278 us -> 120 us (0.43); the launches traced: 274 us -> 120 us
  Pallas kernels: 0 us -> 115 us
  matrix products: 92.8 us -> 0 us
  waiting for transfers between devices: 89.6 us -> 0 us
  local copies, waits for them, and re-layouts: 82.6 us -> 4.7 us
  starting transfers between devices: 8.47 us -> 0 us
    pallas_call x0 -> x1, Pallas kernels: none -> 115 us  [body(): pl.pallas_call(functools.partial(kernel, dims), out_shape=jax.ShapeDtypeS...]
    dot_general x16 -> x0, matrix products: 92.8 us -> none  [the longest x14 73.8 us: mixing(): jnp.einsum('gkj,gjr->gkr', weight, coeffs, precision=lax.Precision.HIGHEST)]
    ppermute x5 -> x0, waiting for transfers between devices: 89.6 us -> none  [from_partner(): return lax.ppermute(value, axis, pairs)]
    unnamed x16 -> x1, local copies, waits for them, and re-layouts: 27.2 us -> 4.7 us
    add x5 -> x0, local copies, waits for them, and re-layouts: 18.6 us -> none  [the longest x4 15 us: body(): coeffs = own_part + mixing(weight[..., rank:], partner)]
    ppermute x5 -> x0, local copies, waits for them, and re-layouts: 14.1 us -> none  [from_partner(): return lax.ppermute(value, axis, pairs)]
    squeeze x1 -> x0, local copies, waits for them, and re-layouts: 11 us -> none  [body(): weight = tgt_weights[:, bit_pos]]
    ppermute x5 -> x0, starting transfers between devices: 8.47 us -> none  [from_partner(): return lax.ppermute(value, axis, pairs)]
  transfers between devices with their start and end apart: 5 -> 0, of which waited for: 4 -> 0; matrix products, arithmetic and copies ran while one was open for 11% -> 0% of each run, Pallas kernels for 0% -> 0%
where the time goes in v1:
time: 120 us
  Pallas kernels  115 us (96%)
  local copies, waits for them, and re-layouts  4.7 us (4%)
    pallas_call x1, Pallas kernels, body(): pl.pallas_call(functools.partial(kernel, dims), out_shape=jax.ShapeDtypeS...  115 us
    unnamed x1, local copies, waits for them, and re-layouts  4.7 us

profile of v1, /device:TPU:0, one launch (start us, length us, event | category | flops | bytes accessed | tf_op | source)
XLA Modules:
  0.0 120.1 jit_solution(17992336520308637118)
XLA Ops:
  0.0 115.4 %shard_map.46 = f32[64,128,128]{2,1,0:T(8,128)} custom-call(f32[64,128,128]{2,1,0:T(8,128)} %sources.1, f32[4096,128]{1,0:T(8,128)} %bitcast.4, f32[4096,128]{1,0:T(8,128)} %bitcast.5, f32[14336,128]{1,0:T(8,128)} %bitcast.3), custom_call_target="tpu_custom_call" | custom-call | tf_op jit(solution)/shard_map/pallas_call | solution.py:248
  115.4 4.7 %copy.6 = f32[64,128,128]{2,1,0:T(8,128)} copy(f32[64,128,128]{2,1,0:T(8,128)} %shard_map.46) | data formatting | bytes 8388608

commit v2 on v1

--- a/solution.py
+++ b/solution.py
@@ -104,15 +104,19 @@
             return
         half = 2**n
 
-        def flip(k, carry):
-            for t in range(tiles):
-                x = c_buf[n, at_chunk(c, k, t), :]
-                low = (lane // half) % 2 == 0
-                p_buf[n, at_chunk(c, k, t), :] = jnp.where(
-                    low, pltpu.roll(x, 128 - half, 1), pltpu.roll(x, half, 1))
+        low = (lane // half) % 2 == 0
+        group = 8
+
+        def flip(outer, carry):
+            places = [at_chunk(c, outer * group + i, t) for i in range(group) for t in range(tiles)]
+            values = [c_buf[n, place, :] for place in places]
+            ahead = [pltpu.roll(x, 128 - half, 1) for x in values]
+            behind = [pltpu.roll(x, half, 1) for x in values]
+            for place, up, down in zip(places, ahead, behind):
+                p_buf[n, place, :] = jnp.where(low, up, down)
             return carry
 
-        lax.fori_loop(0, rank, flip, 0)
+        lax.fori_loop(0, rank // group, flip, 0)
 
     def first(c):
         if c == 0:
@@ -208,7 +212,7 @@
     flight = [0.0] * (levels + 2)
     links = [None] * (levels + 2)
     for e, (axis, bit) in enumerate(partners):
-        flight[local + e + 1] = 0.5 if (axis == "src" and bit == 0) else 5.0
+        flight[local + e + 1] = 0.5 if (axis == "src" and bit == 0) else 4.5
         links[local + e + 1] = (axis, bit) if axis == "tgt" or bit == 0 else axis
     busy, ready, nxt = {}, {(0, c): 0.0 for c in range(chunks)}, {c: 0 for c in range(chunks)}
     now, order = 0.0, []

time: 120 us -> 107 us (0.89)
  Pallas kernels: 115 us -> 102 us
    pallas_call x1, Pallas kernels: 115 us -> 102 us  [body(): pl.pallas_call(functools.partial(kernel, dims), out_shape=jax.ShapeDtypeS...]
where the time goes in v2:
time: 107 us
  Pallas kernels  102 us (95%)
  local copies, waits for them, and re-layouts  4.7 us (4%)
    pallas_call x1, Pallas kernels, body(): pl.pallas_call(functools.partial(kernel, dims), out_shape=jax.ShapeDtypeS...  102 us
    unnamed x1, local copies, waits for them, and re-layouts  4.7 us

profile of v2, /device:TPU:0, one launch (start us, length us, event | category | flops | bytes accessed | tf_op | source)
XLA Modules:
  0.0 106.8 jit_solution(8295425078552426144)
XLA Ops:
  0.0 102.1 %shard_map.46 = f32[64,128,128]{2,1,0:T(8,128)} custom-call(f32[64,128,128]{2,1,0:T(8,128)} %sources.1, f32[4096,128]{1,0:T(8,128)} %bitcast.4, f32[4096,128]{1,0:T(8,128)} %bitcast.5, f32[14336,128]{1,0:T(8,128)} %bitcast.3), custom_call_target="tpu_custom_call" | custom-call | tf_op jit(solution)/shard_map/pallas_call | solution.py:252
  102.1 4.7 %copy.6 = f32[64,128,128]{2,1,0:T(8,128)} copy(f32[64,128,128]{2,1,0:T(8,128)} %shard_map.46) | data formatting | bytes 8388608
